TPU v7x, 32 devices: a whole 2x2x4 slice. The times are simulated.
32 devices in a mesh: groups: 2 (over x), frame: 8 (over z, y), band: 2 (over core).
Axes of the slice: x: 2, y: 2, z: 4, core: 2. Of those that a mesh axis runs over, the one named last changes fastest.
Arguments:
- hidden_in: bfloat16 [16, 1536, 1152], P(('groups', 'frame'), 'band'), parts along dimension 0, may hold values from -6 to 6
- latents: float32 [16, 192, 128], P(('groups', 'frame'), 'band'), parts along dimension 0, may hold values from -6 to 6
- fresh_noise: float32 [384, 128], P(('groups', 'band')), parts along dimension 0, may hold values from -6 to 6
- level_index: int32 [16], P(('groups', 'frame')), parts along dimension 0, may hold values from 1 to 31
- time_table: int32 [32], replicated, may hold values from 0 to 999, as said below
- frame_offset: int32 [2], P('groups'), parts along dimension 0, may hold values from 0 to 1023
- mod_table: float32 [3456], replicated, may hold values from -3 to 3
- time_weight: bfloat16 [128, 3456], replicated, may hold values from -0.5 to 0.5
- spatial_qkv: bfloat16 [1152, 1728], replicated, may hold values from -6 to 6
- spatial_out: bfloat16 [576, 1152], replicated, may hold values from -0.25 to 0.25
- temporal_qkv: bfloat16 [1152, 1728], replicated, may hold values from -6 to 6
- temporal_out: bfloat16 [576, 1152], replicated, may hold values from -0.25 to 0.25
- final_gain: float32 [1152], replicated, may hold values from 0.5 to 1.5
- out_weight: bfloat16 [1152, 16], replicated, may hold values from -0.1875 to 0.1875
Outputs:
- hidden_out: bfloat16 [16, 1536, 1152], P(('groups', 'frame'), 'band'), parts along dimension 0
- velocity: float32 [16, 192, 128], P(('groups', 'frame'), 'band'), parts along dimension 0
- next_latents: float32 [16, 192, 128], P(('groups', 'frame'), 'band'), parts along dimension 0
There are 2 independent parts, one for each index of `groups`. A program takes and returns all parts, laid end to end along the dimension named above; an argument that names none is the same for every part. Nothing has to cross between parts.
Inputs may be any that keep to these rules, and one draw needn't show every extreme that they name: `time_table`: entries rise strictly along the table, from 0 at the first entry to 999 at the last.
All inputs are finite; a program needn't handle non-finite values.
Results may differ from a plain program's by a relative error of at most 0.025.
Values may be sent and summed in bfloat16 or wider, within the bound.
No kernel may reach another device: no remote copies, remote signals or barrier semaphores. Data moves between devices by JAX's collectives and lax.ppermute only.
A program may use at most 128 MiB of HBM per device.

v0:
```python
import math
import jax
import jax.numpy as jnp
from jax import lax
from jax.sharding import PartitionSpec as P

HEAD_SIZE = 72
epsilon = 1e-06


def from_behind(value, axis, steps):
    count = lax.axis_size(axis)
    initial, last = (max(0, -steps), min(count, count - steps))
    return lax.ppermute(value, axis, [(source, source + steps) for source in range(initial, last)])


def layer_norm(values):
    average = jnp.mean(values, axis=-1, keepdims=True)
    centred = values - average
    variance = jnp.mean(centred * centred, axis=-1, keepdims=True)
    return centred * lax.rsqrt(variance + epsilon)


def sinusoid(position, feature_count, first_sine):
    half_width = feature_count // 2
    frequency = jnp.exp(-math.log(10000.0) * jnp.arange(half_width, dtype=jnp.float32) / half_width)
    angles = position.astype(jnp.float32)[:, None] * frequency[None, :]
    if first_sine:
        return jnp.concatenate([jnp.sin(angles), jnp.cos(angles)], axis=-1)
    return jnp.concatenate([jnp.cos(angles), jnp.sin(angles)], axis=-1)


def mix_frames(rows, head_count):
    frame_count = rows.shape[0]
    item_count = rows.shape[1]
    parted = rows.reshape(frame_count, item_count, 3, head_count, HEAD_SIZE)
    attention_scores = jnp.einsum(
        "fnhd,gnhd->nhfg", parted[:, :, 0], parted[:, :, 1], preferred_element_type=jnp.float32
    ) / math.sqrt(HEAD_SIZE)
    row_max = jnp.max(attention_scores, axis=-1, keepdims=True)
    attention_weight = jnp.exp(attention_scores - row_max).astype(jnp.bfloat16)
    denominator = jnp.sum(attention_weight, axis=-1, dtype=jnp.float32)
    weighted_sum = jnp.einsum(
        "nhfg,gnhd->fnhd", attention_weight, parted[:, :, 2], preferred_element_type=jnp.float32
    )
    mixed = weighted_sum / jnp.transpose(denominator, (2, 0, 1))[..., None]
    return mixed.astype(jnp.bfloat16).reshape(frame_count, item_count, head_count * HEAD_SIZE)


def body(
    hidden_in,
    latents,
    fresh_noise,
    level_index,
    time_table,
    frame_offset,
    mod_table,
    time_weight,
    spatial_qkv,
    spatial_out,
    temporal_qkv,
    temporal_out,
    final_gain,
    out_weight,
):
    tokens = hidden_in.shape[1]
    model_width = hidden_in.shape[2]
    attended = spatial_out.shape[0]
    head_count = attended // HEAD_SIZE
    peers = lax.axis_size("frame")
    table_index = jnp.arange(time_table.shape[0], dtype=jnp.int32)
    now_steps = jnp.sum(
        jnp.where(table_index[None, :] == level_index[:, None], time_table[None, :], 0), axis=1
    )
    next_steps = jnp.sum(
        jnp.where(table_index[None, :] == level_index[:, None] - 1, time_table[None, :], 0), axis=1
    )
    activated = jax.nn.silu(sinusoid(now_steps, time_weight.shape[0], False)).astype(jnp.bfloat16)
    modulation = mod_table[None, :] + jnp.dot(
        activated, time_weight, preferred_element_type=jnp.float32
    )
    shift_part = modulation[:, :model_width]
    scale_part = modulation[:, model_width : 2 * model_width]
    gate_part = modulation[:, 2 * model_width :]
    inputs = hidden_in[0].astype(jnp.float32)
    normed = (layer_norm(inputs) * (1.0 + scale_part) + shift_part).astype(jnp.bfloat16)
    projected = jnp.dot(normed, spatial_qkv, preferred_element_type=jnp.float32).astype(
        jnp.bfloat16
    )
    query_rows = projected[:, :attended].reshape(tokens, head_count, HEAD_SIZE)
    key_value = projected[:, attended:]
    block_rows = lax.all_gather(key_value, "band", axis=0, tiled=True)
    row_max = jnp.full((head_count, tokens), -1e30, jnp.float32)
    row_count = block_rows.shape[0]
    key_matrix_rows = block_rows[:, :attended].reshape(row_count, head_count, HEAD_SIZE)
    value_matrix_rows = block_rows[:, attended:].reshape(row_count, head_count, HEAD_SIZE)
    attention_scores = jnp.einsum(
        "ubg,wbg->buw", query_rows, key_matrix_rows, preferred_element_type=jnp.float32
    ) / math.sqrt(HEAD_SIZE)
    new_max = jnp.maximum(row_max, jnp.max(attention_scores, axis=-1))
    attention_weight = jnp.exp(attention_scores - new_max[:, :, None]).astype(jnp.bfloat16)
    denominator = jnp.sum(attention_weight, axis=-1, dtype=jnp.float32)
    weighted_sum = jnp.einsum(
        "leq,qlr->ler", attention_weight, value_matrix_rows, preferred_element_type=jnp.float32
    )
    row_max, denominator, weighted_sum = (new_max, denominator, weighted_sum)
    spatial_mixed = (
        jnp.transpose(weighted_sum / denominator[:, :, None], (1, 0, 2))
        .reshape(tokens, attended)
        .astype(jnp.bfloat16)
    )
    residual = inputs + gate_part * jnp.dot(
        spatial_mixed, spatial_out, preferred_element_type=jnp.float32
    )
    position = lax.axis_index("frame") + frame_offset
    placed = sinusoid(position, model_width, True)
    temporal_in = (residual + placed).astype(jnp.bfloat16)
    spread_rows = temporal_in.reshape(1, peers, tokens // peers, model_width)
    gathered = lax.all_to_all(spread_rows, "frame", split_axis=1, concat_axis=0, tiled=True)
    frame_count = gathered.shape[0]
    item_count = gathered.shape[2]
    rows = jnp.dot(
        gathered.reshape(frame_count * item_count, model_width),
        temporal_qkv,
        preferred_element_type=jnp.float32,
    ).astype(jnp.bfloat16)
    mixed = mix_frames(rows.reshape(frame_count, item_count, 3 * attended), head_count)
    mixed_rows = mixed.reshape(frame_count, 1, item_count, attended)
    mixed_pairs = mixed_rows.reshape(mixed_rows.shape[0], 1, mixed_rows.shape[2] // 2, 2 * attended)
    returned = lax.all_to_all(mixed_pairs, "frame", split_axis=0, concat_axis=1, tiled=True)
    temporal_mixed = returned.reshape(tokens, attended)
    residual = residual + gate_part * jnp.dot(
        temporal_mixed, temporal_out, preferred_element_type=jnp.float32
    )
    hidden_out = residual.astype(jnp.bfloat16)[None]
    final_rows = (layer_norm(residual) * final_gain).astype(jnp.bfloat16)
    velocity = jnp.dot(final_rows, out_weight, preferred_element_type=jnp.float32).reshape(
        1, latents.shape[1], 128
    )
    time_delta = (next_steps - now_steps).astype(jnp.float32) / 1000.0
    update = latents + time_delta[:, None, None] * velocity
    shifted = from_behind(update.astype(jnp.bfloat16), "frame", 1).astype(update.dtype)
    next_latents = jnp.where(lax.axis_index("frame") == 0, fresh_noise[None], shifted)
    return (hidden_out, velocity, next_latents)


def solution(mesh):
    placed = (
        P(("groups", "frame"), "band", None),
        P(("groups", "frame"), "band", None),
        P(("groups", "band"), None),
        P(("groups", "frame")),
        P(),
        P("groups"),
        P(),
        P(),
        P(),
        P(),
        P(),
        P(),
        P(),
        P(),
    )
    return jax.shard_map(
        body,
        mesh=mesh,
        in_specs=placed,
        out_specs=(
            P(("groups", "frame"), "band", None),
            P(("groups", "frame"), "band", None),
            P(("groups", "frame"), "band", None),
        ),
        check_vma=False,
    )
```

profile of v0, /device:TPU:0, one launch (start us, length us, event | category | flops | bytes accessed | tf_op | source)
XLA Modules:
  0.0 232.9 jit_solution(8526192935074219680)
XLA Ops:
  7.2 0.0 copy-start
  7.2 0.0 copy-start.1
  7.2 0.0 all-gather.2.cloned.1.call-start
  8.0 1.4 fusion.32
  10.2 1.5 convolution_reduce_fusion
  11.7 0.7 add.73
  12.5 1.8 convert_reduce_fusion.1
  14.3 0.0 copy-done.1
  14.3 0.6 fusion.6
  14.9 5.9 %convolution_convert_fusion.1 = bf16[768,1728]{0,1:T(8,128)(2,1)S(1)} fusion(bf16[1152,1728]{0,1:T(8,128)(2,1)} %param.22, bf16[1,768,1152]{2,1,0:T(8,128)(2,1)S(1)} %copy-done.1, f32[1152]{0:T(1024)S(1)} %get-tuple-element.4, f32[1152]{0:T(1024)S(1)} %get-tuple-element.5, f32[768]{0:T(1024)S(1)} %add_rsqrt_fusion.1, f32[768]{0:T(1024)S(1)} %broadcast_multiply_fusion.1), kind=kOutput, calls=%fused_computation.21 | convolution fusion | flops 3064283136 | bytes 8420352 | tf_op jit(solution)/shard_map/dot_general | solution.py:87
  20.8 0.0 copy-start.2
  20.8 1.5 copy-done.2
  22.3 1.3 slice.44
  23.6 0.0 all-gather.2.cloned.1.call-update
  24.3 0.1 fusion.29
  24.4 0.1 maximum_reduce_fusion
  24.5 14.7 %all-gather.2.cloned.1.call-done = bf16[1536,1152]{0,1:T(8,128)(2,1)} async-done(((bf16[768,1152]{0,1:T(8,128)(2,1)}), bf16[1536,1152]{0,1:T(8,128)(2,1)}) %all-gather.2.cloned.1.call-update) | async-done | bytes 3538960 | tf_op jit(solution)/shard_map/all_gather | solution.py:92
  39.3 0.0 slice-start
  39.3 3.5 %fusion.45 = (bf16[1536,576]{0,1:T(8,128)(2,1)S(1)}, bf16[1536,576]{0,1:T(8,128)(2,1)}) fusion(bf16[1536,1152]{0,1:T(8,128)(2,1)} %all-gather.2.cloned.1.call-done), kind=kLoop, calls=%fused_computation.79 | loop fusion | bytes 7077888 | tf_op jit(solution)/shard_map/slice | solution.py:95
  42.8 0.0 slice-done
  42.8 14.8 %multiply_reduce_fusion = (f32[8,768]{1,0:T(8,128)S(1)}, f32[8,768,1536]{2,1,0:T(8,128)}) fusion(bf16[768,8,72]{0,2,1:T(8,128)(2,1)S(1)} %bitcast.79, bf16[1536,8,72]{0,2,1:T(8,128)(2,1)S(1)} %bitcast.78), kind=kOutput, calls=%fused_computation.3 | convolution fusion | flops 1377822720 | bytes 40427520 | tf_op jit(solution)/shard_map/ubg,wbg->buw/dot_general | solution.py:97
  57.6 16.7 %convert_reduce_fusion = f32[8,768]{1,0:T(8,128)S(1)} fusion(f32[8,768]{1,0:T(8,128)S(1)} %broadcast_maximum_fusion, f32[8,768,1536]{2,1,0:T(8,128)} %get-tuple-element.16), kind=kLoop, calls=%fused_computation.1 | loop fusion | flops 47179776 | bytes 37797888 | tf_op jit(solution)/shard_map/reduce_sum | solution.py:102
  74.3 16.7 %fusion.13 = bf16[768,8,72]{0,2,1:T(8,128)(2,1)} fusion(bf16[1536,8,72]{0,2,1:T(8,128)(2,1)} %bitcast.81, f32[8,768,1536]{2,1,0:T(8,128)} %get-tuple-element.16, f32[8,768]{1,0:T(8,128)S(1)} %broadcast_maximum_fusion, f32[768,8]{0,1:T(8,128)S(1)} %bitcast.85), kind=kOutput, calls=%fused_computation.26 | convolution fusion | flops 1388150784 | bytes 40452096 | tf_op jit(solution)/shard_map/leq,qlr->ler/dot_general | solution.py:103
  91.0 0.0 copy-done
  91.0 0.0 copy-start.9
  91.0 5.0 %add_convert_fusion = (bf16[768,1152]{1,0:T(8,128)(2,1)S(1)}, f32[768,1152]{1,0:T(8,128)}) fusion(f32[1152]{0:T(1024)S(1)} %maximum_reduce_fusion, bf16[768,576]{0,1:T(8,128)(2,1)} %bitcast.86, bf16[576,1152]{1,0:T(8,128)(2,1)S(1)} %copy-done, f32[1152]{0:T(1024)S(1)} %get-tuple-element.3, bf16[1,768,1152]{2,1,0:T(8,128)(2,1)S(1)} %copy-done.1), kind=kOutput, calls=%fused_computation.19 | convolution fusion | flops 1023639552 | bytes 9298944 | tf_op jit(solution)/shard_map/dot_general | solution.py:112
  95.9 47.3 %all_to_all.8 = bf16[1,8,96,1152]{3,2,0,1:T(8,128)(2,1)S(1)} all-to-all(bf16[1,8,96,1152]{3,2,0,1:T(8,128)(2,1)S(1)} %bitcast.82), channel_id=1, replica_groups=mesh['groups'=2,'frame'=8,'band'=2] {'frame'}, dimensions={1} | all-to-all | bytes 3538944 | tf_op jit(solution)/shard_map/all_to_all | solution.py:119
  143.2 0.0 copy-done.9
  143.2 5.0 %convolution_convert_fusion = bf16[768,1728]{0,1:T(8,128)(2,1)} fusion(bf16[768,1152]{1,0:T(8,128)(2,1)S(1)} %bitcast.83, bf16[1152,1728]{0,1:T(8,128)(2,1)S(1)} %copy-done.9), kind=kOutput, calls=%fused_computation.20 | convolution fusion | flops 3058974720 | bytes 8404992 | tf_op jit(solution)/shard_map/dot_general | solution.py:122
  148.2 7.0 %reshape_reshape.3 = bf16[8,96,3,8,72]{1,0,4,3,2:T(8,128)(2,1)} reshape(bf16[768,1728]{0,1:T(8,128)(2,1)} %convolution_convert_fusion) | data formatting | bytes 5308416 | tf_op jit(solution)/shard_map/reshape;reshape | solution.py:36
  155.2 4.0 %fusion.44 = (bf16[8,96,1,8,72]{1,0,4,3,2:T(8,128)(2,1)}, bf16[8,96,1,8,72]{1,0,4,3,2:T(8,128)(2,1)}, bf16[8,96,1,8,72]{1,0,4,3,2:T(8,128)(2,1)}) fusion(bf16[8,96,3,8,72]{1,0,4,3,2:T(8,128)(2,1)} %reshape_reshape.3), kind=kLoop, calls=%fused_computation.78 | loop fusion | bytes 5308416 | tf_op jit(solution)/shard_map/slice | solution.py:44
  159.2 3.9 %copy.56 = bf16[8,96,1,8,72]{4,0,3,1,2:T(8,128)(2,1)S(1)} copy(bf16[8,96,1,8,72]{1,0,4,3,2:T(8,128)(2,1)} %get-tuple-element.11) | data formatting | bytes 1769472
  163.1 4.6 %copy.57 = bf16[8,96,1,8,72]{4,0,3,1,2:T(8,128)(2,1)} copy(bf16[8,96,1,8,72]{1,0,4,3,2:T(8,128)(2,1)} %get-tuple-element.12) | data formatting | bytes 1769472
  167.6 4.0 %fusion.19 = f32[96,8,8,8]{2,3,1,0:T(8,128)} fusion(bf16[8,96,1,8,72]{4,0,3,1,2:T(8,128)(2,1)} %copy.57, bf16[8,96,1,8,72]{4,0,3,1,2:T(8,128)(2,1)S(1)} %copy.56), kind=kOutput, calls=%fused_computation.33 | convolution fusion | flops 7077888 | bytes 1966080 | tf_op jit(solution)/shard_map/fnhd,gnhd->nhfg/dot_general | solution.py:37
  171.6 0.0 copy-start.3
  171.7 3.2 %copy.48 = f32[96,8,8,8]{0,3,2,1:T(8,128)S(1)} copy(f32[96,8,8,8]{2,3,1,0:T(8,128)} %fusion.19) | data formatting | bytes 393216 | tf_op jit(solution)/shard_map/fnhd,gnhd->nhfg/dot_general | solution.py:37
  174.8 0.2 convert_reduce_fusion.2
  175.0 2.9 %copy.49 = bf16[96,8,8,8]{3,2,1,0:T(8,128)(2,1)} copy(bf16[96,8,8,8]{0,3,2,1:T(8,128)(2,1)S(1)} %get-tuple-element.20) | data formatting | bytes 196608 | tf_op jit(solution)/shard_map/convert_element_type | solution.py:41
  178.0 0.2 copy.50
  178.2 0.0 copy-done.3
  178.2 3.4 %copy.55 = bf16[8,96,1,8,72]{4,0,3,1,2:T(8,128)(2,1)} copy(bf16[8,96,1,8,72]{1,0,4,3,2:T(8,128)(2,1)S(1)} %copy-done.3) | data formatting | bytes 1769472
  181.6 3.0 %fusion.10 = bf16[8,96,8,72]{3,0,2,1:T(8,128)(2,1)S(1)} fusion(bf16[96,8,8,8]{3,2,1,0:T(8,128)(2,1)} %copy.49, bf16[8,96,1,8,72]{4,0,3,1,2:T(8,128)(2,1)} %copy.55, f32[8,96,8]{0,2,1:T(8,128)S(1)} %copy.50), kind=kOutput, calls=%fused_computation.23 | convolution fusion | flops 7962624 | bytes 1892352 | tf_op jit(solution)/shard_map/nhfg,gnhd->fnhd/dot_general | solution.py:43
  184.6 0.2 copy.51
  184.8 2.5 %reshape_reshape_reshape.3 = bf16[8,1,48,1152]{3,2,0,1:T(8,128)(2,1)} reshape(bf16[8,96,8,72]{3,2,1,0:T(8,128)(2,1)S(1)} %copy.51) | data formatting | bytes 1769472 | tf_op jit(solution)/shard_map/reshape;reshape;reshape | solution.py:129
  187.3 3.8 %all-to-all-start.1 = ((bf16[8,1,48,1152]{3,2,1,0:T(8,128)(2,1)}), bf16[8,1,48,1152]{3,2,1,0:T(8,128)(2,1)S(1)}, u32[]{:S(2)}, u32[]{:S(2)}) async-start(bf16[8,1,48,1152]{3,2,1,0:T(8,128)(2,1)} %bitcast.80), calls=%async_computation.1 | async-start | bytes 1769472 | tf_op jit(solution)/shard_map/all_to_all | solution.py:130
  192.4 20.9 %all-to-all-done.1 = bf16[8,1,48,1152]{3,2,1,0:T(8,128)(2,1)S(1)} async-done(((bf16[8,1,48,1152]{3,2,1,0:T(8,128)(2,1)}), bf16[8,1,48,1152]{3,2,1,0:T(8,128)(2,1)S(1)}, u32[]{:S(2)}, u32[]{:S(2)}) %all-to-all-start.1) | async-done | bytes 884768 | tf_op jit(solution)/shard_map/all_to_all | solution.py:130
  213.3 0.6 reshape.171
  213.9 4.1 %fusion.46 = (f32[768]{0:T(1024)S(1)}, f32[768,1152]{1,0:T(8,128)S(1)}) fusion(f32[768,1152]{1,0:T(8,128)} %get-tuple-element.18, bf16[768,576]{1,0:T(8,128)(2,1)S(1)} %reshape.171, bf16[576,1152]{1,0:T(8,128)(2,1)} %param.25, f32[1152]{0:T(1024)S(1)} %get-tuple-element.3), kind=kOutput, calls=%fused_computation.80 | convolution fusion | flops 1021869312 | bytes 9297408 | tf_op jit(solution)/shard_map/dot_general | solution.py:132
  218.0 0.0 copy-start.7
  218.0 0.0 copy-start.8
  218.1 1.8 multiply_reduce_fusion.1
  219.9 0.0 copy-start.5
  219.9 0.0 copy-start.6
  219.9 0.0 copy-done.7
  219.9 0.0 copy-done.8
  219.9 0.7 fusion.18
  220.6 0.2 reshape.172
  220.8 0.0 copy-done.5
  220.8 0.0 copy-start.4
  220.8 3.1 %collective-permute-start = (bf16[1,96,128]{2,1,0:T(8,128)(2,1)S(1)}, bf16[1,96,128]{2,1,0:T(8,128)(2,1)S(1)}, u32[]{:S(2)}, u32[]{:S(2)}) collective-permute-start(bf16[1,96,128]{2,1,0:T(8,128)(2,1)S(1)} %add_convert_fusion.1), channel_id=1, source_target_pairs={{0,2},{2,4},{4,6},{6,8},{8,10},{10,12},{12,14},{1,3},{3,5},{5,7},{... | collective-permute-start | bytes 73736 | tf_op jit(solution)/shard_map/ppermute | solution.py:14
  224.0 1.5 collective-permute-done
  225.5 0.0 copy-done.6
  225.5 0.6 bitcast_select_fusion
  226.1 0.0 copy-done.4
  (9 shorter events, 0.1 us)
Async XLA Ops:
  7.2 83.8 %copy-start = (bf16[576,1152]{1,0:T(8,128)(2,1)S(1)}, bf16[576,1152]{1,0:T(8,128)(2,1)}, u32[]{:S(2)}) copy-start(bf16[576,1152]{1,0:T(8,128)(2,1)} %param.23) | copy-start | bytes 3981316
  7.2 7.1 %copy-start.1 = (bf16[1,768,1152]{2,1,0:T(8,128)(2,1)S(1)}, bf16[1,768,1152]{2,1,0:T(8,128)(2,1)}, u32[]{:S(2)}) copy-start(bf16[1,768,1152]{2,1,0:T(8,128)(2,1)} %param.14) | copy-start | bytes 5308420
  7.2 32.1 %all-gather.2.cloned.1.call-start = ((), (), s32[]{:S(2)}) async-start(), calls=%async_computation.2 | async-start | bytes 5308416 | tf_op jit(solution)/shard_map/all_gather | solution.py:92
  20.8 1.5 copy-start.2
  39.3 3.5 %slice-start = ((bf16[768,1728]{0,1:T(8,128)(2,1)}), bf16[768,576]{0,1:T(8,128)(2,1)S(1)}, s32[]{:S(2)}) async-start(bf16[768,1728]{0,1:T(8,128)(2,1)} %copy-done.2), calls=%async_computation.3 | async-start | bytes 1769472 | tf_op jit(solution)/shard_map/slice | solution.py:90
  91.0 52.3 %copy-start.9 = (bf16[1152,1728]{0,1:T(8,128)(2,1)S(1)}, bf16[1152,1728]{0,1:T(8,128)(2,1)}, u32[]{:S(2)}) copy-start(bf16[1152,1728]{0,1:T(8,128)(2,1)} %param.24) | copy-start | bytes 11943940
  171.6 6.5 %copy-start.3 = (bf16[8,96,1,8,72]{1,0,4,3,2:T(8,128)(2,1)S(1)}, bf16[8,96,1,8,72]{1,0,4,3,2:T(8,128)(2,1)}, u32[]{:S(2)}) copy-start(bf16[8,96,1,8,72]{1,0,4,3,2:T(8,128)(2,1)} %get-tuple-element.10) | copy-start | bytes 2654212
  187.3 26.0 %all-to-all-start.1 = ((bf16[8,1,48,1152]{3,2,1,0:T(8,128)(2,1)}), bf16[8,1,48,1152]{3,2,1,0:T(8,128)(2,1)S(1)}, u32[]{:S(2)}, u32[]{:S(2)}) async-start(bf16[8,1,48,1152]{3,2,1,0:T(8,128)(2,1)} %bitcast.80), calls=%async_computation.1 | async-start | bytes 1769472 | tf_op jit(solution)/shard_map/all_to_all | solution.py:130
  218.0 1.9 copy-start.7
  218.0 1.9 copy-start.8
  219.9 0.9 copy-start.5
  219.9 5.6 %copy-start.6 = (f32[96,128]{1,0:T(8,128)S(1)}, f32[96,128]{1,0:T(8,128)}, u32[]{:S(2)}) copy-start(f32[96,128]{1,0:T(8,128)} %param.16) | copy-start | bytes 147460
  220.8 5.3 %copy-start.4 = (f32[1,96,128]{2,1,0:T(8,128)}, f32[1,96,128]{2,1,0:T(8,128)S(1)}, u32[]{:S(2)}) copy-start(f32[1,96,128]{2,1,0:T(8,128)S(1)} %reshape.172) | copy-start | bytes 147460
  220.8 4.6 %collective-permute-start = (bf16[1,96,128]{2,1,0:T(8,128)(2,1)S(1)}, bf16[1,96,128]{2,1,0:T(8,128)(2,1)S(1)}, u32[]{:S(2)}, u32[]{:S(2)}) collective-permute-start(bf16[1,96,128]{2,1,0:T(8,128)(2,1)S(1)} %add_convert_fusion.1), channel_id=1, source_target_pairs={{0,2},{2,4},{4,6},{6,8},{8,10},{10,12},{12,14},{1,3},{3,5},{5,7},{... | collective-permute-start | bytes 73736 | tf_op jit(solution)/shard_map/ppermute | solution.py:14
Sparse Core Ops, SparseCore 0:
  23.8 15.4 all-gather.1
where the time goes:
time: 234 us; the launch traced here: 233 us
  matrix products  60.7 us (26%)
  blocking collectives  47.3 us (20%)
  local copies, waits for them, and re-layouts  38.9 us (17%)
  waiting for transfers between devices  37.1 us (16%)
  other arithmetic  24.2 us (10%)
  between operations  17.7 us (8%)
  starting transfers between devices  6.96 us (3%)
    all_to_all x1, blocking collectives, body(): lax.all_to_all(spread_rows, 'frame', split_axis=1, concat_axis=0, tiled=T...  47.3 us
    all_to_all x1, waiting for transfers between devices, body(): lax.all_to_all(mixed_pairs, 'frame', split_axis=0, concat_axis=1, tiled=T...  20.9 us
    reduce_sum x1, other arithmetic, body(): denominator = jnp.sum(attention_weight, axis=-1, dtype=jnp.float32)  16.7 us
    dot_general x1, matrix products, body(): jnp.einsum('leq,qlr->ler', attention_weight, value_matrix_rows, preferred...  16.7 us
    dot_general x1, matrix products, body(): jnp.einsum('ubg,wbg->buw', query_rows, key_matrix_rows, preferred_element...  14.8 us
    all_gather x1, waiting for transfers between devices, body(): block_rows = lax.all_gather(key_value, 'band', axis=0, tiled=True)  14.7 us
    unnamed x23, local copies, waits for them, and re-layouts  13.4 us
    another operation x1, local copies, waits for them, and re-layouts, mix_frames(): parted = rows.reshape(frame_count, item_count, 3, head_count, HEAD_SIZE)  6.97 us
  transfers between devices with their start and end apart: 3, of which 3 were waited for; matrix products, arithmetic and copies ran while one was open for 0% of the time, Pallas kernels for 0%

commit v1 on v0

--- a/solution.py
+++ b/solution.py
@@ -127,7 +127,10 @@
     mixed = mix_frames(rows.reshape(frame_count, item_count, 3 * attended), head_count)
     mixed_rows = mixed.reshape(frame_count, 1, item_count, attended)
     mixed_pairs = mixed_rows.reshape(mixed_rows.shape[0], 1, mixed_rows.shape[2] // 2, 2 * attended)
-    returned = lax.all_to_all(mixed_pairs, "frame", split_axis=0, concat_axis=1, tiled=True)
+    returned = jnp.concatenate(
+        lax.all_to_all(jnp.stack(jnp.split(mixed_pairs, lax.axis_size("frame"), 0)), "frame", 0, 0),
+        1,
+    )
     temporal_mixed = returned.reshape(tokens, attended)
     residual = residual + gate_part * jnp.dot(
         temporal_mixed, temporal_out, preferred_element_type=jnp.float32

time: 234 us -> 248 us (1.060)
  local copies, waits for them, and re-layouts: 38.9 us -> 52.7 us
    split x0 -> x1, local copies, waits for them, and re-layouts: none -> 9.47 us  [body(): jnp.split(mixed_pairs, lax.axis_size('frame'), 0)]
    unnamed x23 -> x30, local copies, waits for them, and re-layouts: 13.4 us -> 18 us
where the time goes in v1:
time: 248 us; the launch traced here: 247 us
  matrix products  60.7 us (24%)
  local copies, waits for them, and re-layouts  52.7 us (21%)
  blocking collectives  47.3 us (19%)
  waiting for transfers between devices  37.3 us (15%)
  other arithmetic  24.2 us (10%)
  between operations  17.7 us (7%)
  starting transfers between devices  6.84 us (3%)
    all_to_all x1, blocking collectives, body(): lax.all_to_all(spread_rows, 'frame', split_axis=1, concat_axis=0, tiled=T...  47.3 us
    all_to_all x1, waiting for transfers between devices, body(): lax.all_to_all(jnp.stack(jnp.split(mixed_pairs, lax.axis_size('frame'), 0...  21 us
    unnamed x30, local copies, waits for them, and re-layouts  18 us
    reduce_sum x1, other arithmetic, body(): denominator = jnp.sum(attention_weight, axis=-1, dtype=jnp.float32)  16.7 us
    dot_general x1, matrix products, body(): jnp.einsum('leq,qlr->ler', attention_weight, value_matrix_rows, preferred...  16.7 us
    dot_general x1, matrix products, body(): jnp.einsum('ubg,wbg->buw', query_rows, key_matrix_rows, preferred_element...  14.8 us
    all_gather x1, waiting for transfers between devices, body(): block_rows = lax.all_gather(key_value, 'band', axis=0, tiled=True)  14.7 us
    split x1, local copies, waits for them, and re-layouts, body(): jnp.split(mixed_pairs, lax.axis_size('frame'), 0)  9.47 us
  transfers between devices with their start and end apart: 3, of which 3 were waited for; matrix products, arithmetic and copies ran while one was open for 0% of the time, Pallas kernels for 0%

profile of v1, /device:TPU:0, one launch (start us, length us, event | category | flops | bytes accessed | tf_op | source)
XLA Modules:
  0.0 246.7 jit_solution(10925627177147007724)
XLA Ops:
  7.2 0.0 copy-start
  7.2 0.0 copy-start.1
  7.2 0.0 all-gather.2.cloned.1.call-start
  8.0 1.4 fusion.32
  10.2 1.5 convolution_reduce_fusion
  11.7 0.7 add.73
  12.5 1.8 convert_reduce_fusion.1
  14.3 0.6 fusion.6
  14.9 5.9 %convolution_convert_fusion.1 = bf16[768,1728]{0,1:T(8,128)(2,1)S(1)} fusion(bf16[1152,1728]{0,1:T(8,128)(2,1)} %param.22, bf16[1,768,1152]{2,1,0:T(8,128)(2,1)S(1)} %copy-done.1, f32[1152]{0:T(1024)S(1)} %get-tuple-element.12, f32[1152]{0:T(1024)S(1)} %get-tuple-element.13, f32[768]{0:T(1024)S(1)} %add_rsqrt_fusion.1, f32[768]{0:T(1024)S(1)} %broadcast_multiply_fusion.1), kind=kOutput, calls=%fused_computation.21 | convolution fusion | flops 3064283136 | bytes 8420352 | tf_op jit(solution)/shard_map/dot_general | solution.py:87
  20.8 1.5 copy-done.2
  22.3 1.3 slice.52
  23.6 0.0 all-gather.2.cloned.1.call-update
  24.3 0.1 fusion.29
  24.4 0.1 maximum_reduce_fusion
  24.5 14.7 %all-gather.2.cloned.1.call-done = bf16[1536,1152]{0,1:T(8,128)(2,1)} async-done(((bf16[768,1152]{0,1:T(8,128)(2,1)}), bf16[1536,1152]{0,1:T(8,128)(2,1)}) %all-gather.2.cloned.1.call-update) | async-done | bytes 3538960 | tf_op jit(solution)/shard_map/all_gather | solution.py:92
  39.3 3.5 %fusion.45 = (bf16[1536,576]{0,1:T(8,128)(2,1)S(1)}, bf16[1536,576]{0,1:T(8,128)(2,1)}) fusion(bf16[1536,1152]{0,1:T(8,128)(2,1)} %all-gather.2.cloned.1.call-done), kind=kLoop, calls=%fused_computation.95 | loop fusion | bytes 7077888 | tf_op jit(solution)/shard_map/slice | solution.py:95
  42.8 14.8 %multiply_reduce_fusion = (f32[8,768]{1,0:T(8,128)S(1)}, f32[8,768,1536]{2,1,0:T(8,128)}) fusion(bf16[768,8,72]{0,2,1:T(8,128)(2,1)S(1)} %bitcast.76, bf16[1536,8,72]{0,2,1:T(8,128)(2,1)S(1)} %bitcast.75), kind=kOutput, calls=%fused_computation.3 | convolution fusion | flops 1377822720 | bytes 40427520 | tf_op jit(solution)/shard_map/ubg,wbg->buw/dot_general | solution.py:97
  57.6 16.7 %convert_reduce_fusion = f32[8,768]{1,0:T(8,128)S(1)} fusion(f32[8,768]{1,0:T(8,128)S(1)} %broadcast_maximum_fusion, f32[8,768,1536]{2,1,0:T(8,128)} %get-tuple-element.24), kind=kLoop, calls=%fused_computation.1 | loop fusion | flops 47179776 | bytes 37797888 | tf_op jit(solution)/shard_map/reduce_sum | solution.py:102
  74.3 16.7 %fusion.13 = bf16[768,8,72]{0,2,1:T(8,128)(2,1)} fusion(bf16[1536,8,72]{0,2,1:T(8,128)(2,1)} %bitcast.77, f32[8,768,1536]{2,1,0:T(8,128)} %get-tuple-element.24, f32[8,768]{1,0:T(8,128)S(1)} %broadcast_maximum_fusion, f32[768,8]{0,1:T(8,128)S(1)} %bitcast.81), kind=kOutput, calls=%fused_computation.26 | convolution fusion | flops 1388150784 | bytes 40452096 | tf_op jit(solution)/shard_map/leq,qlr->ler/dot_general | solution.py:103
  91.0 5.0 %add_convert_fusion = (bf16[768,1152]{1,0:T(8,128)(2,1)S(1)}, f32[768,1152]{1,0:T(8,128)}) fusion(f32[1152]{0:T(1024)S(1)} %maximum_reduce_fusion, bf16[768,576]{0,1:T(8,128)(2,1)} %bitcast.82, bf16[576,1152]{1,0:T(8,128)(2,1)S(1)} %copy-done, f32[1152]{0:T(1024)S(1)} %get-tuple-element.11, bf16[1,768,1152]{2,1,0:T(8,128)(2,1)S(1)} %copy-done.1), kind=kOutput, calls=%fused_computation.19 | convolution fusion | flops 1023639552 | bytes 9298944 | tf_op jit(solution)/shard_map/dot_general | solution.py:112
  95.9 47.3 %all_to_all.14 = bf16[1,8,96,1152]{3,2,0,1:T(8,128)(2,1)S(1)} all-to-all(bf16[1,8,96,1152]{3,2,0,1:T(8,128)(2,1)S(1)} %bitcast.78), channel_id=1, replica_groups=mesh['groups'=2,'frame'=8,'band'=2] {'frame'}, dimensions={1} | all-to-all | bytes 3538944 | tf_op jit(solution)/shard_map/all_to_all | solution.py:119
  143.2 5.0 %convolution_convert_fusion = bf16[768,1728]{0,1:T(8,128)(2,1)} fusion(bf16[768,1152]{1,0:T(8,128)(2,1)S(1)} %bitcast.79, bf16[1152,1728]{0,1:T(8,128)(2,1)S(1)} %copy-done.9), kind=kOutput, calls=%fused_computation.20 | convolution fusion | flops 3058974720 | bytes 8404992 | tf_op jit(solution)/shard_map/dot_general | solution.py:122
  148.2 7.0 %reshape_reshape.6 = bf16[8,96,3,8,72]{1,0,4,3,2:T(8,128)(2,1)} reshape(bf16[768,1728]{0,1:T(8,128)(2,1)} %convolution_convert_fusion) | data formatting | bytes 5308416 | tf_op jit(solution)/shard_map/reshape;reshape | solution.py:36
  155.2 4.0 %fusion.44 = (bf16[8,96,1,8,72]{1,0,4,3,2:T(8,128)(2,1)}, bf16[8,96,1,8,72]{1,0,4,3,2:T(8,128)(2,1)}, bf16[8,96,1,8,72]{1,0,4,3,2:T(8,128)(2,1)}) fusion(bf16[8,96,3,8,72]{1,0,4,3,2:T(8,128)(2,1)} %reshape_reshape.6), kind=kLoop, calls=%fused_computation.94 | loop fusion | bytes 5308416 | tf_op jit(solution)/shard_map/slice | solution.py:44
  159.2 3.9 %copy.49 = bf16[8,96,1,8,72]{4,0,3,1,2:T(8,128)(2,1)S(1)} copy(bf16[8,96,1,8,72]{1,0,4,3,2:T(8,128)(2,1)} %get-tuple-element.19) | data formatting | bytes 1769472
  163.1 4.6 %copy.50 = bf16[8,96,1,8,72]{4,0,3,1,2:T(8,128)(2,1)} copy(bf16[8,96,1,8,72]{1,0,4,3,2:T(8,128)(2,1)} %get-tuple-element.20) | data formatting | bytes 1769472
  167.6 4.0 %fusion.19 = f32[96,8,8,8]{2,3,1,0:T(8,128)} fusion(bf16[8,96,1,8,72]{4,0,3,1,2:T(8,128)(2,1)} %copy.50, bf16[8,96,1,8,72]{4,0,3,1,2:T(8,128)(2,1)S(1)} %copy.49), kind=kOutput, calls=%fused_computation.33 | convolution fusion | flops 7077888 | bytes 1966080 | tf_op jit(solution)/shard_map/fnhd,gnhd->nhfg/dot_general | solution.py:37
  171.7 3.2 %copy.43 = f32[96,8,8,8]{0,3,2,1:T(8,128)S(1)} copy(f32[96,8,8,8]{2,3,1,0:T(8,128)} %fusion.19) | data formatting | bytes 393216 | tf_op jit(solution)/shard_map/fnhd,gnhd->nhfg/dot_general | solution.py:37
  174.8 0.2 convert_reduce_fusion.2
  175.0 2.9 %copy.44 = bf16[96,8,8,8]{3,2,1,0:T(8,128)(2,1)} copy(bf16[96,8,8,8]{0,3,2,1:T(8,128)(2,1)S(1)} %get-tuple-element.28) | data formatting | bytes 196608 | tf_op jit(solution)/shard_map/convert_element_type | solution.py:41
  178.0 0.2 copy.45
  178.2 0.0 copy-done.3
  178.2 3.4 %copy.48 = bf16[8,96,1,8,72]{4,0,3,1,2:T(8,128)(2,1)} copy(bf16[8,96,1,8,72]{1,0,4,3,2:T(8,128)(2,1)S(1)} %copy-done.3) | data formatting | bytes 1769472
  181.6 3.0 %fusion.10 = bf16[8,96,8,72]{3,0,2,1:T(8,128)(2,1)S(1)} fusion(bf16[96,8,8,8]{3,2,1,0:T(8,128)(2,1)} %copy.44, bf16[8,96,1,8,72]{4,0,3,1,2:T(8,128)(2,1)} %copy.48, f32[8,96,8]{0,2,1:T(8,128)S(1)} %copy.45), kind=kOutput, calls=%fused_computation.23 | convolution fusion | flops 7962624 | bytes 1892352 | tf_op jit(solution)/shard_map/nhfg,gnhd->fnhd/dot_general | solution.py:43
  184.6 9.5 %slice_reduce_fusion = (bf16[96,8,72]{2,1,0:T(8,128)(2,1)S(1)}, bf16[96,8,72]{2,1,0:T(8,128)(2,1)S(1)}, bf16[96,8,72]{2,1,0:T(8,128)(2,1)S(1)}, bf16[96,8,72]{2,...) fusion(bf16[8,96,8,72]{3,0,2,1:T(8,128)(2,1)S(1)} %fusion.10), kind=kLoop, calls=%fused_computation.41 | loop fusion | bytes 1769472 | tf_op jit(solution)/shard_map/split | solution.py:131
  194.1 0.2 stack.27
  194.3 0.7 constant_dynamic-update-slice_fusion.7
  194.9 0.2 stack.28
  195.2 0.2 stack.29
  195.4 0.2 stack.30
  195.6 0.2 stack.31
  195.9 0.2 stack.32
  196.1 0.2 stack.33
  196.3 0.2 stack.34
  196.5 0.7 constant_dynamic-update-slice_fusion.6
  197.2 0.7 constant_dynamic-update-slice_fusion.5
  197.9 0.7 constant_dynamic-update-slice_fusion.4
  198.5 0.7 constant_dynamic-update-slice_fusion.3
  199.2 0.7 constant_dynamic-update-slice_fusion.2
  199.8 0.7 constant_dynamic-update-slice_fusion.1
  200.5 0.7 constant_dynamic-update-slice_fusion
  201.1 3.6 %all-to-all-start.1 = ((bf16[8,1,1,48,1152]{4,3,2,1,0:T(8,128)(2,1)}), bf16[8,1,1,48,1152]{4,3,2,1,0:T(8,128)(2,1)S(1)}, u32[]{:S(2)}, u32[]{:S(2)}) async-start(bf16[8,1,1,48,1152]{4,3,2,1,0:T(8,128)(2,1)} %constant_dynamic-update-slice_fusion), calls=%async_computation.1 | async-start | bytes 1769472 | tf_op jit(solution)/shard_map/all_to_all | solution.py:131
  206.0 21.0 %all-to-all-done.1 = bf16[8,1,1,48,1152]{4,3,2,1,0:T(8,128)(2,1)S(1)} async-done(((bf16[8,1,1,48,1152]{4,3,2,1,0:T(8,128)(2,1)}), bf16[8,1,1,48,1152]{4,3,2,1,0:T(8,128)(2,1)S(1)}, u32[]{:S(2)}, u32[]{:S(2)}) %all-to-all-start.1) | async-done | bytes 884768 | tf_op jit(solution)/shard_map/all_to_all | solution.py:131
  227.0 0.6 reshape_reshape.7
  227.6 4.1 %fusion.46 = (f32[768]{0:T(1024)S(1)}, f32[768,1152]{1,0:T(8,128)S(1)}) fusion(f32[768,1152]{1,0:T(8,128)} %get-tuple-element.26, bf16[768,576]{1,0:T(8,128)(2,1)S(1)} %reshape_reshape.7, bf16[576,1152]{1,0:T(8,128)(2,1)} %param.25, f32[1152]{0:T(1024)S(1)} %get-tuple-element.11), kind=kOutput, calls=%fused_computation.96 | convolution fusion | flops 1021869312 | bytes 9297408 | tf_op jit(solution)/shard_map/dot_general | solution.py:135
  231.7 0.0 copy-start.7
  231.7 0.0 copy-start.8
  231.7 1.8 multiply_reduce_fusion.1
  233.6 0.7 fusion.18
  234.3 0.2 reshape.180
  234.5 0.0 copy-start.4
  234.5 3.2 %collective-permute-start = (bf16[1,96,128]{2,1,0:T(8,128)(2,1)S(1)}, bf16[1,96,128]{2,1,0:T(8,128)(2,1)S(1)}, u32[]{:S(2)}, u32[]{:S(2)}) collective-permute-start(bf16[1,96,128]{2,1,0:T(8,128)(2,1)S(1)} %add_convert_fusion.1), channel_id=1, source_target_pairs={{0,2},{2,4},{4,6},{6,8},{8,10},{10,12},{12,14},{1,3},{3,5},{5,7},{... | collective-permute-start | bytes 73736 | tf_op jit(solution)/shard_map/ppermute | solution.py:14
  237.8 1.5 collective-permute-done
  239.3 0.6 bitcast_select_fusion
  (24 shorter events, 0.2 us)
Async XLA Ops:
  7.2 83.8 %copy-start = (bf16[576,1152]{1,0:T(8,128)(2,1)S(1)}, bf16[576,1152]{1,0:T(8,128)(2,1)}, u32[]{:S(2)}) copy-start(bf16[576,1152]{1,0:T(8,128)(2,1)} %param.23) | copy-start | bytes 3981316
  7.2 7.1 %copy-start.1 = (bf16[1,768,1152]{2,1,0:T(8,128)(2,1)S(1)}, bf16[1,768,1152]{2,1,0:T(8,128)(2,1)}, u32[]{:S(2)}) copy-start(bf16[1,768,1152]{2,1,0:T(8,128)(2,1)} %param.14) | copy-start | bytes 5308420
  7.2 32.1 %all-gather.2.cloned.1.call-start = ((), (), s32[]{:S(2)}) async-start(), calls=%async_computation.2 | async-start | bytes 5308416 | tf_op jit(solution)/shard_map/all_gather | solution.py:92
  20.8 1.5 copy-start.2
  39.3 3.5 %slice-start = ((bf16[768,1728]{0,1:T(8,128)(2,1)}), bf16[768,576]{0,1:T(8,128)(2,1)S(1)}, s32[]{:S(2)}) async-start(bf16[768,1728]{0,1:T(8,128)(2,1)} %copy-done.2), calls=%async_computation.3 | async-start | bytes 1769472 | tf_op jit(solution)/shard_map/slice | solution.py:90
  91.0 52.3 %copy-start.9 = (bf16[1152,1728]{0,1:T(8,128)(2,1)S(1)}, bf16[1152,1728]{0,1:T(8,128)(2,1)}, u32[]{:S(2)}) copy-start(bf16[1152,1728]{0,1:T(8,128)(2,1)} %param.24) | copy-start | bytes 11943940
  171.6 6.5 %copy-start.3 = (bf16[8,96,1,8,72]{1,0,4,3,2:T(8,128)(2,1)S(1)}, bf16[8,96,1,8,72]{1,0,4,3,2:T(8,128)(2,1)}, u32[]{:S(2)}) copy-start(bf16[8,96,1,8,72]{1,0,4,3,2:T(8,128)(2,1)} %get-tuple-element.18) | copy-start | bytes 2654212
  201.1 25.9 %all-to-all-start.1 = ((bf16[8,1,1,48,1152]{4,3,2,1,0:T(8,128)(2,1)}), bf16[8,1,1,48,1152]{4,3,2,1,0:T(8,128)(2,1)S(1)}, u32[]{:S(2)}, u32[]{:S(2)}) async-start(bf16[8,1,1,48,1152]{4,3,2,1,0:T(8,128)(2,1)} %constant_dynamic-update-slice_fusion), calls=%async_computation.1 | async-start | bytes 1769472 | tf_op jit(solution)/shard_map/all_to_all | solution.py:131
  231.7 1.9 copy-start.7
  231.7 1.9 copy-start.8
  233.5 0.9 copy-start.5
  233.5 5.7 %copy-start.6 = (f32[96,128]{1,0:T(8,128)S(1)}, f32[96,128]{1,0:T(8,128)}, u32[]{:S(2)}) copy-start(f32[96,128]{1,0:T(8,128)} %param.16) | copy-start | bytes 147460
  234.5 5.4 %copy-start.4 = (f32[1,96,128]{2,1,0:T(8,128)}, f32[1,96,128]{2,1,0:T(8,128)S(1)}, u32[]{:S(2)}) copy-start(f32[1,96,128]{2,1,0:T(8,128)S(1)} %reshape.180) | copy-start | bytes 147460
  234.5 4.8 %collective-permute-start = (bf16[1,96,128]{2,1,0:T(8,128)(2,1)S(1)}, bf16[1,96,128]{2,1,0:T(8,128)(2,1)S(1)}, u32[]{:S(2)}, u32[]{:S(2)}) collective-permute-start(bf16[1,96,128]{2,1,0:T(8,128)(2,1)S(1)} %add_convert_fusion.1), channel_id=1, source_target_pairs={{0,2},{2,4},{4,6},{6,8},{8,10},{10,12},{12,14},{1,3},{3,5},{5,7},{... | collective-permute-start | bytes 73736 | tf_op jit(solution)/shard_map/ppermute | solution.py:14
Sparse Core Ops, SparseCore 0:
  23.8 15.4 all-gather.1
